TPU v7x, 8 devices: a whole 2x2x1 slice. The times are simulated.
8 devices in a mesh: data: 1 (over z), dap: 8 (over y, x, core).
Axes of the slice: x: 2, y: 2, z: 1, core: 2. Of those that a mesh axis runs over, the one named last changes fastest.
Arguments:
- z_one: bfloat16 [768, 768, 128], P(('data', 'dap'))
- mask_one: int32 [768, 768], P(('data', 'dap'))
- z_two: bfloat16 [768, 768, 128], P(('data', 'dap'))
- mask_two: int32 [768, 768], P(('data', 'dap'))
- norm_in: bfloat16 [2, 2, 128], replicated
- w_proj: bfloat16 [2, 128, 512], replicated
- w_gate: bfloat16 [2, 128, 128], replicated
- norm_mid: bfloat16 [2, 2, 128], replicated
- w_out: bfloat16 [2, 128, 128], replicated
Outputs:
- output 1: bfloat16 [768, 768, 128], P(('data', 'dap'))
- output 2: bfloat16 [768, 768, 128], P(('data', 'dap'))
All inputs are finite; a program needn't handle non-finite values.
Results may differ from a plain program's by a relative error of at most 0.00659121.
Values are sent between devices in bfloat16 or wider.
A program may use at most 1 GiB of HBM per device.

v0:
```python
import jax
import jax.numpy as jnp
from jax import lax
from jax.sharding import PartitionSpec as P


def layer_norm(vals, ln_gain, ln_shift, feature_axis):
    vals = vals.astype(jnp.float32)
    row_mean = jnp.mean(vals, axis=feature_axis, keepdims=True)
    centred = vals - row_mean
    row_var = jnp.mean(centred * centred, axis=feature_axis, keepdims=True)
    return centred * lax.rsqrt(row_var + 1e-5) * ln_gain.astype(jnp.float32) + ln_shift.astype(jnp.float32)


def project_rows(z_rows, mask_rows, norm_in, w_proj):
    pair_width = z_rows.shape[2]
    hidden = w_proj.shape[1] // 4
    x_norm = layer_norm(z_rows, norm_in[0], norm_in[1], -1).astype(jnp.bfloat16)
    w_split = w_proj.reshape(pair_width, 2, 2, hidden)
    projected = jnp.einsum("rnz,zsgc->sgcrn", x_norm, w_split, preferred_element_type=jnp.float32)
    keep_mask = mask_rows.astype(jnp.float32)
    sides = (keep_mask * jax.nn.sigmoid(projected[:, 1]) * projected[:, 0]).astype(jnp.bfloat16)
    return x_norm, sides


def finish_rows(z_rows, x_norm, t_rows, w_gate, norm_mid, w_out):
    t_norm = layer_norm(t_rows, norm_mid[0][:, None, None], norm_mid[1][:, None, None], 0).astype(jnp.bfloat16)
    update = jnp.einsum("crn,cz->rnz", t_norm, w_out, preferred_element_type=jnp.float32)
    gate_val = jax.nn.sigmoid(jnp.einsum("rnz,zy->rny", x_norm, w_gate, preferred_element_type=jnp.float32))
    return (z_rows.astype(jnp.float32) + gate_val * update).astype(jnp.bfloat16)


def tri_update(z_rows, mask_rows, norm_in, w_proj, w_gate, norm_mid, w_out, form):
    x_norm, sides = project_rows(z_rows, mask_rows, norm_in, w_proj)
    sides_chan = lax.all_to_all(sides, "dap", 1, 2, tiled=True)
    tri_prod = jnp.einsum(form, sides_chan[0], sides_chan[1], preferred_element_type=jnp.float32).astype(jnp.bfloat16)
    t_rows = lax.all_to_all(tri_prod, "dap", 1, 0, tiled=True)
    return finish_rows(z_rows, x_norm, t_rows, w_gate, norm_mid, w_out)


def solution(mesh):
    row_spec = P(("data", "dap"), None, None)
    mask_spec = P(("data", "dap"), None)
    replicated = P()

    def crop_update(z_rows, mask_rows, norm_in, w_proj, w_gate, norm_mid, w_out):
        z_mid = tri_update(z_rows, mask_rows, norm_in[0], w_proj[0], w_gate[0], norm_mid[0], w_out[0], "cik,cjk->cij")
        return tri_update(z_mid, mask_rows, norm_in[1], w_proj[1], w_gate[1], norm_mid[1], w_out[1], "cki,ckj->cij")

    def per_device(z_one, mask_one, z_two, mask_two, norm_in, w_proj, w_gate, norm_mid, w_out):
        return (crop_update(z_one, mask_one, norm_in, w_proj, w_gate, norm_mid, w_out),
                crop_update(z_two, mask_two, norm_in, w_proj, w_gate, norm_mid, w_out))

    return jax.shard_map(per_device, mesh=mesh,
                         in_specs=(row_spec, mask_spec, row_spec, mask_spec, replicated, replicated, replicated, replicated, replicated),
                         out_specs=(row_spec, row_spec), check_vma=False)
```

profile of v0, /device:TPU:0, one launch (start us, length us, event | category | flops | bytes accessed | tf_op | source)
XLA Modules:
  0.0 3326.6 jit_solution(6958897969242156072)
XLA Ops:
  43.2 57.1 %convolution_bitcast_fusion.3 = f32[2,2,128,96,768]{2,4,1,0,3:T(8,128)} fusion(bf16[128,2,2,128,1]{0,3,2,1,4:T(8,128)(2,1)S(1)} %bitcast.301, bf16[96,768,128]{1,2,0:T(8,128)(2,1)} %copy.153, f32[128]{0:T(128)S(1)} %get-tuple-element.29, f32[128]{0:T(128)S(1)} %get-tuple-element.30, f32[96,768]{1,0:T(8,128)S(1)} %add_rsqrt_fusion.7, ...), kind=kOutput, calls=%fused_computation.52 | convolution fusion | flops 9720299520 | bytes 170591232 | tf_op jit(solution)/shard_map/rnz,zsgc->sgcrn/dot_general | solution.py:20
  100.3 59.1 %fusion.22 = bf16[2,128,96,768]{1,3,0,2:T(8,128)(2,1)} fusion(f32[2,2,128,96,768]{2,4,1,0,3:T(8,128)} %convolution_bitcast_fusion.3, f32[96,768]{1,0:T(8,128)S(1)} %convert_element_type.206), kind=kLoop, calls=%fused_computation.29 | loop fusion | flops 113246208 | bytes 189038592 | tf_op jit(solution)/shard_map/convert_element_type | solution.py:22
  159.5 91.8 %copy.160 = bf16[2,128,96,768]{3,0,2,1:T(2,128)(2,1)} copy(bf16[2,128,96,768]{1,3,0,2:T(8,128)(2,1)} %fusion.22) | data formatting | bytes 75497472 | tf_op jit(solution)/shard_map/convert_element_type | solution.py:22
  298.8 57.1 %convolution_bitcast_fusion.1 = f32[2,2,128,96,768]{2,4,0,3,1:T(8,128)} fusion(bf16[128,2,2,128,1]{0,3,2,1,4:T(8,128)(2,1)S(1)} %bitcast.302, bf16[96,768,128]{1,2,0:T(8,128)(2,1)} %copy.185, f32[96,768]{1,0:T(8,128)S(1)} %add_rsqrt_fusion.3, f32[96,768]{1,0:T(8,128)S(1)} %broadcast_multiply_fusion.3, f32[128]{0:T(128)S(1)} %get-tuple-element.29, ...), kind=kOutput, calls=%fused_computation.50 | convolution fusion | flops 9720299520 | bytes 170591232 | tf_op jit(solution)/shard_map/rnz,zsgc->sgcrn/dot_general | solution.py:20
  356.0 59.1 %fusion.8 = bf16[2,128,96,768]{1,3,0,2:T(8,128)(2,1)} fusion(f32[2,2,128,96,768]{2,4,0,3,1:T(8,128)} %convolution_bitcast_fusion.1, f32[96,768]{1,0:T(8,128)S(1)} %convert_element_type.235), kind=kLoop, calls=%fused_computation.11 | loop fusion | flops 113246208 | bytes 189038592 | tf_op jit(solution)/shard_map/convert_element_type | solution.py:22
  415.1 92.0 %copy.190 = bf16[2,128,96,768]{3,0,2,1:T(2,128)(2,1)} copy(bf16[2,128,96,768]{1,3,0,2:T(8,128)(2,1)} %fusion.8) | data formatting | bytes 75497472 | tf_op jit(solution)/shard_map/convert_element_type | solution.py:22
  507.1 160.6 %all-to-all-done = bf16[2,128,96,768]{3,0,2,1:T(2,128)(2,1)} async-done(((bf16[2,128,96,768]{3,0,2,1:T(2,128)(2,1)}), bf16[2,128,96,768]{3,0,2,1:T(2,128)(2,1)}, u32[]{:S(2)}, u32[]{:S(2)}) %all-to-all-start) | async-done | bytes 37748768 | tf_op jit(solution)/shard_map/all_to_all | solution.py:35
  751.7 30.9 convolution_convert_fusion.3
  802.7 280.4 %all-to-all-done.4 = bf16[2,128,96,768]{3,0,2,1:T(2,128)(2,1)} async-done(((bf16[2,128,96,768]{3,0,2,1:T(2,128)(2,1)}), bf16[2,128,96,768]{3,0,2,1:T(2,128)(2,1)}, u32[]{:S(2)}, u32[]{:S(2)}) %all-to-all-start.4) | async-done | bytes 37748768 | tf_op jit(solution)/shard_map/all_to_all | solution.py:35
  1166.7 31.0 convolution_convert_fusion.1
  1217.9 76.5 %all-to-all-done.1 = bf16[16,768,768]{2,0,1:T(8,128)(2,1)} async-done(((bf16[16,768,768]{2,0,1:T(8,128)(2,1)}), bf16[16,768,768]{2,0,1:T(8,128)(2,1)}, u32[]{:S(2)}, u32[]{:S(2)}) %all-to-all-start.1) | async-done | bytes 18874400 | tf_op jit(solution)/shard_map/all_to_all | solution.py:37
  1337.3 168.7 %all-to-all-done.5 = bf16[16,768,768]{2,0,1:T(8,128)(2,1)} async-done(((bf16[16,768,768]{2,0,1:T(8,128)(2,1)}), bf16[16,768,768]{2,0,1:T(8,128)(2,1)}, u32[]{:S(2)}, u32[]{:S(2)}) %all-to-all-start.5) | async-done | bytes 18874400 | tf_op jit(solution)/shard_map/all_to_all | solution.py:37
  1522.4 26.3 fusion.72
  1566.1 33.2 convert_reduce_fusion.2
  1608.0 57.2 %convolution_bitcast_fusion.2 = f32[2,2,128,96,768]{2,4,0,3,1:T(8,128)} fusion(bf16[128,2,2,128,1]{0,3,2,1,4:T(8,128)(2,1)S(1)} %bitcast.299, bf16[96,768,128]{1,2,0:T(8,128)(2,1)} %get-tuple-element.35, f32[128]{0:T(128)S(1)} %copy-done.37, f32[128]{0:T(128)S(1)} %copy-done.34, f32[96,768]{1,0:T(8,128)S(1)} %add_rsqrt_fusion.5, ...), kind=kOutput, calls=%fused_computation.51 | convolution fusion | flops 9720299520 | bytes 170591232 | tf_op jit(solution)/shard_map/rnz,zsgc->sgcrn/dot_general | solution.py:20
  1665.2 59.1 %fusion.15 = bf16[2,128,96,768]{1,3,0,2:T(8,128)(2,1)} fusion(f32[2,2,128,96,768]{2,4,0,3,1:T(8,128)} %convolution_bitcast_fusion.2, f32[96,768]{1,0:T(8,128)S(1)} %copy-done.19), kind=kLoop, calls=%fused_computation.20 | loop fusion | flops 113246208 | bytes 189038592 | tf_op jit(solution)/shard_map/convert_element_type | solution.py:22
  1724.3 91.8 %copy.173 = bf16[2,128,96,768]{3,0,2,1:T(2,128)(2,1)} copy(bf16[2,128,96,768]{1,3,0,2:T(8,128)(2,1)} %fusion.15) | data formatting | bytes 75497472 | tf_op jit(solution)/shard_map/convert_element_type | solution.py:22
  1860.5 33.6 %convert_reduce_fusion = (f32[96,768]{1,0:T(8,128)S(1)}, bf16[96,768,128]{1,2,0:T(8,128)(2,1)}) fusion(bf16[128,96,768]{2,0,1:T(8,128)(2,1)} %bitcast.290, bf16[2,128,128]{2,1,0:T(8,128)(2,1)S(1)} %copy-done.41, f32[96,768,128]{1,2,0:T(8,128)} %fusion.102, bf16[96,768,128]{1,2,0:T(8,128)(2,1)} %copy.185), kind=kOutput, calls=%fused_computation.39 | convolution fusion | flops 2500780032 | bytes 94699520 | tf_op jit(solution)/shard_map/crn,cz->rnz/dot_general | solution.py:28
  1902.8 57.1 %convolution_bitcast_fusion = f32[2,2,128,96,768]{2,4,0,3,1:T(8,128)} fusion(bf16[128,2,2,128,1]{0,3,2,1,4:T(8,128)(2,1)S(1)} %bitcast.300, bf16[96,768,128]{1,2,0:T(8,128)(2,1)} %get-tuple-element.33, f32[96,768]{1,0:T(8,128)S(1)} %add_rsqrt_fusion.1, f32[96,768]{1,0:T(8,128)S(1)} %broadcast_multiply_fusion.1, f32[128]{0:T(128)S(1)} %copy-done.38, ...), kind=kOutput, calls=%fused_computation.49 | convolution fusion | flops 9720299520 | bytes 170591232 | tf_op jit(solution)/shard_map/rnz,zsgc->sgcrn/dot_general | solution.py:20
  1960.0 59.1 %fusion.1 = bf16[2,128,96,768]{1,3,0,2:T(8,128)(2,1)} fusion(f32[2,2,128,96,768]{2,4,0,3,1:T(8,128)} %convolution_bitcast_fusion, f32[96,768]{1,0:T(8,128)S(1)} %copy-done.15), kind=kLoop, calls=%fused_computation.2 | loop fusion | flops 113246208 | bytes 189038592 | tf_op jit(solution)/shard_map/convert_element_type | solution.py:22
  2019.0 92.0 %copy.201 = bf16[2,128,96,768]{3,0,2,1:T(2,128)(2,1)} copy(bf16[2,128,96,768]{1,3,0,2:T(8,128)(2,1)} %fusion.1) | data formatting | bytes 75497472 | tf_op jit(solution)/shard_map/convert_element_type | solution.py:22
  2111.1 120.4 %all-to-all-done.2 = bf16[2,128,96,768]{3,0,2,1:T(2,128)(2,1)} async-done(((bf16[2,128,96,768]{3,0,2,1:T(2,128)(2,1)}), bf16[2,128,96,768]{3,0,2,1:T(2,128)(2,1)}, u32[]{:S(2)}, u32[]{:S(2)}) %all-to-all-start.2) | async-done | bytes 37748768 | tf_op jit(solution)/shard_map/all_to_all | solution.py:35
  2315.4 27.4 convolution_convert_fusion.2
  2362.9 283.9 %all-to-all-done.6 = bf16[2,128,96,768]{3,0,2,1:T(2,128)(2,1)} async-done(((bf16[2,128,96,768]{3,0,2,1:T(2,128)(2,1)}), bf16[2,128,96,768]{3,0,2,1:T(2,128)(2,1)}, u32[]{:S(2)}, u32[]{:S(2)}) %all-to-all-start.6) | async-done | bytes 37748768 | tf_op jit(solution)/shard_map/all_to_all | solution.py:35
  2730.6 27.5 convolution_convert_fusion
  2778.1 80.2 %all-to-all-done.3 = bf16[16,768,768]{2,0,1:T(8,128)(2,1)} async-done(((bf16[16,768,768]{2,0,1:T(8,128)(2,1)}), bf16[16,768,768]{2,0,1:T(8,128)(2,1)}, u32[]{:S(2)}, u32[]{:S(2)}) %all-to-all-start.3) | async-done | bytes 18874400 | tf_op jit(solution)/shard_map/all_to_all | solution.py:37
  2888.2 181.3 %all-to-all-done.7 = bf16[16,768,768]{2,0,1:T(8,128)(2,1)} async-done(((bf16[16,768,768]{2,0,1:T(8,128)(2,1)}), bf16[16,768,768]{2,0,1:T(8,128)(2,1)}, u32[]{:S(2)}, u32[]{:S(2)}) %all-to-all-start.7) | async-done | bytes 18874400 | tf_op jit(solution)/shard_map/all_to_all | solution.py:37
  3094.7 26.3 fusion.64
  3138.2 26.7 fusion.93
  3165.0 34.1 %fusion.56 = bf16[96,768,128]{1,2,0:T(8,128)(2,1)} fusion(bf16[96,768,128]{1,2,0:T(8,128)(2,1)} %get-tuple-element.33, f32[96,768,128]{1,2,0:T(8,128)} %fusion.93, bf16[2,128,128]{2,1,0:T(8,128)(2,1)S(1)} %copy-done.45, f32[96,768]{1,0:T(8,128)S(1)} %copy-done.21, f32[96,768]{1,0:T(8,128)S(1)} %copy-done.13, f32[128]{0:T(128)S(1)} %copy-done.39, ...), kind=kOutput, calls=%fused_computation.80 | convolution fusion | flops 2538602496 | bytes 94995456 | tf_op jit(solution)/shard_map/rnz,zy->rny/dot_general | solution.py:29
  3240.7 26.8 fusion.95
  3267.4 34.4 %fusion.54 = bf16[96,768,128]{1,2,0:T(8,128)(2,1)} fusion(bf16[96,768,128]{1,2,0:T(8,128)(2,1)} %get-tuple-element.35, f32[96,768,128]{1,2,0:T(8,128)} %fusion.95, bf16[2,128,128]{2,1,0:T(8,128)(2,1)S(1)} %copy-done.45, f32[128]{0:T(128)S(1)} %copy-done.39, f32[128]{0:T(128)S(1)} %copy-done.36, f32[96,768]{1,0:T(8,128)S(1)} %copy-done.17, ...), kind=kOutput, calls=%fused_computation.78 | convolution fusion | flops 2538602496 | bytes 94995456 | tf_op jit(solution)/shard_map/rnz,zy->rny/dot_general | solution.py:29
  (227 shorter events, 781.8 us)
Async XLA Ops:
  33.1 67.3 %copy-start.4 = (f32[96,768]{1,0:T(8,128)}, f32[96,768]{1,0:T(8,128)S(1)}, u32[]{:S(2)}) copy-start(f32[96,768]{1,0:T(8,128)S(1)} %broadcast_multiply_fusion.7) | copy-start | bytes 884740
  41.7 58.6 %copy-start.8 = (f32[96,768]{1,0:T(8,128)}, f32[96,768]{1,0:T(8,128)S(1)}, u32[]{:S(2)}) copy-start(f32[96,768]{1,0:T(8,128)S(1)} %add_rsqrt_fusion.7) | copy-start | bytes 884740
  42.4 256.5 %copy-start.28 = (f32[128]{0:T(128)}, f32[128]{0:T(128)S(1)}, u32[]{:S(2)}) copy-start(f32[128]{0:T(128)S(1)} %get-tuple-element.29) | copy-start | bytes 1540
  42.4 256.5 %copy-start.31 = (f32[128]{0:T(128)}, f32[128]{0:T(128)S(1)}, u32[]{:S(2)}) copy-start(f32[128]{0:T(128)S(1)} %get-tuple-element.30) | copy-start | bytes 1540
  43.2 57.1 %copy-start.18 = (f32[96,768]{1,0:T(8,128)}, f32[96,768]{1,0:T(8,128)S(1)}, u32[]{:S(2)}) copy-start(f32[96,768]{1,0:T(8,128)S(1)} %convert_element_type.206) | copy-start | bytes 884740
  251.3 416.4 %all-to-all-start = ((bf16[2,128,96,768]{3,0,2,1:T(2,128)(2,1)}), bf16[2,128,96,768]{3,0,2,1:T(2,128)(2,1)}, u32[]{:S(2)}, u32[]{:S(2)}) async-start(bf16[2,128,96,768]{3,0,2,1:T(2,128)(2,1)} %copy.160), calls=%async_computation | async-start | bytes 75497472 | tf_op jit(solution)/shard_map/all_to_all | solution.py:35
  282.4 73.6 %copy-start.14 = (f32[96,768]{1,0:T(8,128)}, f32[96,768]{1,0:T(8,128)S(1)}, u32[]{:S(2)}) copy-start(f32[96,768]{1,0:T(8,128)S(1)} %convert_element_type.235) | copy-start | bytes 884740
  290.2 65.8 %copy-start.2 = (f32[96,768]{1,0:T(8,128)}, f32[96,768]{1,0:T(8,128)S(1)}, u32[]{:S(2)}) copy-start(f32[96,768]{1,0:T(8,128)S(1)} %broadcast_multiply_fusion.3) | copy-start | bytes 884740
  298.8 57.1 %copy-start.6 = (f32[96,768]{1,0:T(8,128)}, f32[96,768]{1,0:T(8,128)S(1)}, u32[]{:S(2)}) copy-start(f32[96,768]{1,0:T(8,128)S(1)} %add_rsqrt_fusion.3) | copy-start | bytes 884740
  667.7 415.4 %all-to-all-start.4 = ((bf16[2,128,96,768]{3,0,2,1:T(2,128)(2,1)}), bf16[2,128,96,768]{3,0,2,1:T(2,128)(2,1)}, u32[]{:S(2)}, u32[]{:S(2)}) async-start(bf16[2,128,96,768]{3,0,2,1:T(2,128)(2,1)} %copy.190), calls=%async_computation.4 | async-start | bytes 75497472 | tf_op jit(solution)/shard_map/all_to_all | solution.py:35
  1083.1 211.3 %all-to-all-start.1 = ((bf16[16,768,768]{2,0,1:T(8,128)(2,1)}), bf16[16,768,768]{2,0,1:T(8,128)(2,1)}, u32[]{:S(2)}, u32[]{:S(2)}) async-start(bf16[16,768,768]{2,0,1:T(8,128)(2,1)} %copy.164), calls=%async_computation.1 | async-start | bytes 37748736 | tf_op jit(solution)/shard_map/all_to_all | solution.py:37
  1197.7 101.9 %copy-start.47 = (bf16[2,2,128]{2,1,0:T(2,128)(2,1)S(1)}, bf16[2,2,128]{2,1,0:T(2,128)(2,1)}, u32[]{:S(2)}) copy-start(bf16[2,2,128]{2,1,0:T(2,128)(2,1)} %param.16) | copy-start | bytes 3076
  1197.7 102.6 %copy-start.24 = (bf16[1,128,512]{2,1,0:T(8,128)(2,1)S(1)}, bf16[1,128,512]{2,1,0:T(8,128)(2,1)}, u32[]{:S(2)}) copy-start(bf16[1,128,512]{2,1,0:T(8,128)(2,1)} %get-tuple-element.22) | copy-start | bytes 393220
  1197.7 102.7 %copy-start.5 = (f32[96,768]{1,0:T(8,128)S(1)}, f32[96,768]{1,0:T(8,128)}, u32[]{:S(2)}) copy-start(f32[96,768]{1,0:T(8,128)} %copy-done.4) | copy-start | bytes 884740
  1197.7 102.8 %copy-start.9 = (f32[96,768]{1,0:T(8,128)S(1)}, f32[96,768]{1,0:T(8,128)}, u32[]{:S(2)}) copy-start(f32[96,768]{1,0:T(8,128)} %copy-done.8) | copy-start | bytes 884740
  1197.7 102.8 %copy-start.29 = (f32[128]{0:T(128)S(1)}, f32[128]{0:T(128)}, u32[]{:S(2)}) copy-start(f32[128]{0:T(128)} %copy-done.28) | copy-start | bytes 1540
  1197.7 102.8 %copy-start.32 = (f32[128]{0:T(128)S(1)}, f32[128]{0:T(128)}, u32[]{:S(2)}) copy-start(f32[128]{0:T(128)} %copy-done.31) | copy-start | bytes 1540
  1197.7 102.8 %copy-start.43 = (bf16[2,128,128]{2,1,0:T(8,128)(2,1)S(1)}, bf16[2,128,128]{2,1,0:T(8,128)(2,1)}, u32[]{:S(2)}) copy-start(bf16[2,128,128]{2,1,0:T(8,128)(2,1)} %param.15) | copy-start | bytes 196612
  1294.4 211.6 %all-to-all-start.5 = ((bf16[16,768,768]{2,0,1:T(8,128)(2,1)}), bf16[16,768,768]{2,0,1:T(8,128)(2,1)}, u32[]{:S(2)}, u32[]{:S(2)}) async-start(bf16[16,768,768]{2,0,1:T(8,128)(2,1)} %copy.194), calls=%async_computation.5 | async-start | bytes 37748736 | tf_op jit(solution)/shard_map/all_to_all | solution.py:37
  1300.5 307.4 %copy-start.22 = (bf16[1,128,512]{1,2,0:T(8,128)(2,1)}, bf16[1,128,512]{1,2,0:T(8,128)(2,1)S(1)}, u32[]{:S(2)}) copy-start(bf16[1,128,512]{1,2,0:T(8,128)(2,1)S(1)} %copy.253) | copy-start | bytes 393220
  1599.3 65.9 %copy-start.10 = (f32[96,768]{1,0:T(8,128)}, f32[96,768]{1,0:T(8,128)S(1)}, u32[]{:S(2)}) copy-start(f32[96,768]{1,0:T(8,128)S(1)} %broadcast_multiply_fusion.5) | copy-start | bytes 884740
  1607.9 57.2 %copy-start.16 = (f32[96,768]{1,0:T(8,128)}, f32[96,768]{1,0:T(8,128)S(1)}, u32[]{:S(2)}) copy-start(f32[96,768]{1,0:T(8,128)S(1)} %add_rsqrt_fusion.5) | copy-start | bytes 884740
  1608.0 57.2 %copy-start.19 = (f32[96,768]{1,0:T(8,128)S(1)}, f32[96,768]{1,0:T(8,128)}, u32[]{:S(2)}) copy-start(f32[96,768]{1,0:T(8,128)} %copy-done.18) | copy-start | bytes 884740
  1816.1 415.3 %all-to-all-start.2 = ((bf16[2,128,96,768]{3,0,2,1:T(2,128)(2,1)}), bf16[2,128,96,768]{3,0,2,1:T(2,128)(2,1)}, u32[]{:S(2)}, u32[]{:S(2)}) async-start(bf16[2,128,96,768]{3,0,2,1:T(2,128)(2,1)} %copy.173), calls=%async_computation.2 | async-start | bytes 75497472 | tf_op jit(solution)/shard_map/all_to_all | solution.py:35
  1894.1 65.8 %copy-start.12 = (f32[96,768]{1,0:T(8,128)}, f32[96,768]{1,0:T(8,128)S(1)}, u32[]{:S(2)}) copy-start(f32[96,768]{1,0:T(8,128)S(1)} %broadcast_multiply_fusion.1) | copy-start | bytes 884740
  1902.8 57.2 %copy-start.20 = (f32[96,768]{1,0:T(8,128)}, f32[96,768]{1,0:T(8,128)S(1)}, u32[]{:S(2)}) copy-start(f32[96,768]{1,0:T(8,128)S(1)} %add_rsqrt_fusion.1) | copy-start | bytes 884740
  1902.8 57.1 %copy-start.15 = (f32[96,768]{1,0:T(8,128)S(1)}, f32[96,768]{1,0:T(8,128)}, u32[]{:S(2)}) copy-start(f32[96,768]{1,0:T(8,128)} %copy-done.14) | copy-start | bytes 884740
  2231.4 415.3 %all-to-all-start.6 = ((bf16[2,128,96,768]{3,0,2,1:T(2,128)(2,1)}), bf16[2,128,96,768]{3,0,2,1:T(2,128)(2,1)}, u32[]{:S(2)}, u32[]{:S(2)}) async-start(bf16[2,128,96,768]{3,0,2,1:T(2,128)(2,1)} %copy.201), calls=%async_computation.6 | async-start | bytes 75497472 | tf_op jit(solution)/shard_map/all_to_all | solution.py:35
  2646.8 211.5 %all-to-all-start.3 = ((bf16[16,768,768]{2,0,1:T(8,128)(2,1)}), bf16[16,768,768]{2,0,1:T(8,128)(2,1)}, u32[]{:S(2)}, u32[]{:S(2)}) async-start(bf16[16,768,768]{2,0,1:T(8,128)(2,1)} %copy.178), calls=%async_computation.3 | async-start | bytes 37748736 | tf_op jit(solution)/shard_map/all_to_all | solution.py:37
  2758.1 105.0 %copy-start.49 = (f32[128]{0:T(128)S(1)}, f32[128]{0:T(128)}, u32[]{:S(2)}) copy-start(f32[128]{0:T(128)} %get-tuple-element.10) | copy-start | bytes 1540
  2758.1 105.2 %copy-start.48 = (f32[128]{0:T(128)S(1)}, f32[128]{0:T(128)}, u32[]{:S(2)}) copy-start(f32[128]{0:T(128)} %get-tuple-element.13) | copy-start | bytes 1540
  2858.2 211.3 %all-to-all-start.7 = ((bf16[16,768,768]{2,0,1:T(8,128)(2,1)}), bf16[16,768,768]{2,0,1:T(8,128)(2,1)}, u32[]{:S(2)}, u32[]{:S(2)}) async-start(bf16[16,768,768]{2,0,1:T(8,128)(2,1)} %copy.206), calls=%async_computation.7 | async-start | bytes 37748736 | tf_op jit(solution)/shard_map/all_to_all | solution.py:37
  (46 other events, 1046.8 us)
where the time goes:
time: 3350 us; the launch traced here: 3330 us
  waiting for transfers between devices  1350 us (40%)
  local copies, waits for them, and re-layouts  961 us (29%)
  matrix products  575 us (17%)
  other arithmetic  391 us (12%)
  starting transfers between devices  45.5 us (1%)
    all_to_all x4, waiting for transfers between devices, tri_update(): sides_chan = lax.all_to_all(sides, 'dap', 1, 2, tiled=True)  845 us
    all_to_all x4, waiting for transfers between devices, tri_update(): t_rows = lax.all_to_all(tri_prod, 'dap', 1, 0, tiled=True)  507 us
    convert_element_type x4, local copies, waits for them, and re-layouts, project_rows(): (keep_mask * jax.nn.sigmoid(projected[:, 1]) * projected[:, 0]).astype(jn...  368 us
    convert_element_type x4, other arithmetic, project_rows(): (keep_mask * jax.nn.sigmoid(projected[:, 1]) * projected[:, 0]).astype(jn...  236 us
    dot_general x4, matrix products, project_rows(): jnp.einsum('rnz,zsgc->sgcrn', x_norm, w_split, preferred_element_type=jnp...  229 us
    slice x8, local copies, waits for them, and re-layouts, tri_update(): sides_chan[1]  130 us
    dot_general x4, matrix products, finish_rows(): jnp.einsum('crn,cz->rnz', t_norm, w_out, preferred_element_type=jnp.float32)  120 us
    dot_general x4, matrix products, tri_update(): jnp.einsum(form, sides_chan[0], sides_chan[1], preferred_element_type=jnp...  117 us
  transfers between devices with their start and end apart: 8, of which 8 were waited for; matrix products, arithmetic and copies ran while one was open for 33% of the time, Pallas kernels for 0%

commit v1 on v0

v1 whole, which is shorter than its diff:
```python
import functools

import jax
import jax.numpy as jnp
from jax import lax
from jax.experimental import pallas as pl
from jax.experimental.pallas import tpu as pltpu
from jax.sharding import PartitionSpec as P

BF, F32 = jnp.bfloat16, jnp.float32
IB = 16
ST = 17
VMEM = 60 << 20


def norm_cols(vals, gain, shift):
    cen = vals - jnp.mean(vals, axis=0, keepdims=True)
    var = jnp.mean(cen * cen, axis=0, keepdims=True)
    return cen * lax.rsqrt(var + 1e-5) * gain + shift


def put_row(scr, i, side):
    for t in range(side.shape[1] // 128):
        scr[t, pl.ds(i, 128, stride=ST), :] = side[:, t * 128:(t + 1) * 128]


def drain(scr, out):
    for c in range(128):
        for t in range(out.shape[2] // 128):
            out[c, :, t * 128:(t + 1) * 128] = scr[t, c * ST:c * ST + IB, :].astype(BF)


def gated(q):
    return q[:128] * jnp.tanh(q[128:256]) + q[:128], q[256:384] * jnp.tanh(q[384:]) + q[256:384]


def dot(lhs, rhs):
    return jnp.dot(lhs, rhs, preferred_element_type=F32)


def params(*sem):
    return pltpu.CompilerParams(vmem_limit_bytes=VMEM, dimension_semantics=sem)


def proj_kernel(z_ref, m_ref, gain, shift, w_ref, *rest):
    a_ref, b_ref, sa, sb = rest[-4:]
    for i in range(IB):
        x = norm_cols(z_ref[i].T.astype(F32), gain[...], shift[...])
        a, b = gated(dot(w_ref[...], (x * m_ref[i:i + 1, :].astype(F32)).astype(BF)))
        put_row(sa, i, a)
        put_row(sb, i, b)
    drain(sa, a_ref)
    drain(sb, b_ref)


def proj(z, m, gain, shift, w, total, off, prev=()):
    rows, n, _ = z.shape
    kb = 256
    full = lambda shape: pl.BlockSpec(shape, lambda i, j: (0,) * len(shape))
    out = pl.BlockSpec((128, IB, kb), lambda i, j: (0, off // IB + i, j))
    return pl.pallas_call(
        proj_kernel, grid=(rows // IB, n // kb),
        in_specs=[pl.BlockSpec((IB, kb, 128), lambda i, j: (i, j, 0)),
                  pl.BlockSpec((IB, kb), lambda i, j: (i, j)),
                  full((128, kb)), full((128, kb)), full((512, 128))]
        + [pl.BlockSpec(memory_space=pl.ANY)] * len(prev),
        out_specs=[out, out],
        scratch_shapes=[pltpu.VMEM((kb // 128, 128 * ST, 128), F32)] * 2,
        out_shape=[jax.ShapeDtypeStruct((128, total, n), BF)] * 2,
        input_output_aliases={5 + k: k for k in range(len(prev))},
        compiler_params=params("arbitrary", "arbitrary"), name="proj")(z, m, gain, shift, w, *prev)


def tri_out_kernel(n_lhs, sc, *refs):
    lhs, rhs, out, buf = refs[:n_lhs], refs[n_lhs:n_lhs + 4], refs[n_lhs + 4], refs[n_lhs + 5]
    for g in range(out.shape[0]):
        for k, r in enumerate(rhs):
            buf[g, pl.ds(pl.multiple_of(sc[k] * 96, 16), 96), :] = r[g, 0]
        row = 0
        for l in lhs:
            m = l.shape[1]
            out[g, row:row + m, :] = lax.dot_general(
                l[g], buf[g], (((1,), (1,)), ((), ())), preferred_element_type=F32).astype(BF)
            row += m


def tri_out(sc, lhs, rhs):
    cb = 2
    n = lhs[0].shape[2]
    rows = sum(l.shape[1] for l in lhs)

    def rhs_spec(idx):
        return pl.BlockSpec((cb, 1, 96, n), lambda g, s: (g, 0 if idx is None else s[idx], 0, 0))

    return pl.pallas_call(
        functools.partial(tri_out_kernel, len(lhs)),
        grid_spec=pltpu.PrefetchScalarGridSpec(
            num_scalar_prefetch=1, grid=(128 // cb,),
            in_specs=[pl.BlockSpec((cb, l.shape[1], n), lambda g, s: (g, 0, 0)) for l in lhs]
            + [rhs_spec(i) for _, i in rhs],
            out_specs=pl.BlockSpec((cb, rows, 384), lambda g, s: (g, 0, 0)),
            scratch_shapes=[pltpu.VMEM((cb, 384, n), BF)]),
        out_shape=jax.ShapeDtypeStruct((128, rows, 384), BF),
        compiler_params=params("arbitrary"), name="tri_out")(
            sc, *lhs, *[r.reshape(128, r.shape[1] // 96, 96, n) for r, _ in rhs])


def stage_t(t_ref, st):
    for c in range(128):
        st[c * ST:c * ST + IB, :] = t_ref[c].astype(F32)


def pair_t(st, i):
    return jnp.concatenate([st[pl.ds(i, 128, stride=ST), :], st[pl.ds(i + 1, 128, stride=ST), :]], axis=1)


def mid_kernel(sc, t_ref, z_ref, m_ref, n_ref, wg, wo, w2, zm_ref, a_ref, b_ref, st, sa, sb):
    stage_t(t_ref, st)
    for i in range(0, IB, 2):
        zt = jnp.concatenate([z_ref[i].T, z_ref[i + 1].T], axis=1).astype(F32)
        gate = dot(wg[...], norm_cols(zt, n_ref[0], n_ref[1]).astype(BF))
        upd = dot(wo[...], norm_cols(pair_t(st, i), n_ref[2], n_ref[3]).astype(BF))
        zm = (zt + (upd * jnp.tanh(gate) + upd)).astype(BF)
        zm_ref[i], zm_ref[i + 1] = zm[:, :128], zm[:, 128:]
        keep = jnp.concatenate([m_ref[i:i + 1, :], m_ref[i + 1:i + 2, :]], axis=1).astype(F32)
        x2 = norm_cols(zm.astype(F32), n_ref[4], n_ref[5]) * keep
        a, b = gated(dot(w2[...], x2.astype(BF)))
        for r in range(2):
            put_row(sa, i + r, a[:, r * 128:(r + 1) * 128])
            put_row(sb, i + r, b[:, r * 128:(r + 1) * 128])
    drain(sa, a_ref)
    drain(sb, b_ref)


def mid(sc, half, t, t_row, z, m, norms, wg, wo, w2):
    rows = z.shape[0]
    full = lambda a: pl.BlockSpec(a.shape, lambda i, j, s: (0,) * a.ndim)
    side = pl.BlockSpec((128, IB, 128), lambda i, j, s: (0, i, j))
    return pl.pallas_call(
        mid_kernel,
        grid_spec=pltpu.PrefetchScalarGridSpec(
            num_scalar_prefetch=1, grid=(rows // IB, 3),
            in_specs=[pl.BlockSpec((128, IB, 128), lambda i, j, s: (0, t_row // IB + i, j)),
                      pl.BlockSpec((IB, 128, 128), lambda i, j, s: (i, 3 * s[half] + j, 0)),
                      pl.BlockSpec((IB, 128), lambda i, j, s: (i, 3 * s[half] + j)),
                      full(norms), full(wg), full(wo), full(w2)],
            out_specs=[pl.BlockSpec((IB, 128, 128), lambda i, j, s: (i, 0, j)), side, side],
            scratch_shapes=[pltpu.VMEM((128 * ST, 128), F32)] + [pltpu.VMEM((1, 128 * ST, 128), F32)] * 2),
        out_shape=[jax.ShapeDtypeStruct((rows, 128, 384), BF)] + [jax.ShapeDtypeStruct((128, rows, 384), BF)] * 2,
        compiler_params=params("arbitrary", "arbitrary"), name="mid")(sc, t, z, m, norms, wg, wo, w2)


def tri_in_kernel(ns, sel_a, off, sel_b, sc, *refs):
    out, abuf, bbuf = refs[-3:]
    ins = refs[:-3]

    def fill(buf, base, g):
        row = 0
        for r in ins[base * ns:(base + 2) * ns]:
            buf[row:row + r.shape[1], :] = r[g]
            row += r.shape[1]

    def product(g, lo):
        at = abuf[:, lo:lo + 256].T
        rows = at[lo // 2:lo // 2 + 192]
        out[g] = dot(rows, bbuf[...]).astype(BF)

    for g in range(out.shape[0]):
        if sel_a is None:
            fill(abuf, 0, g)
        else:
            pl.when(sc[sel_a] == 0)(lambda: fill(abuf, 0, g))
            pl.when(sc[sel_a] == 1)(lambda: fill(abuf, 2, g))
        nb = 2 if sel_a is None else 4
        pl.when(sc[sel_b] == 0)(lambda: fill(bbuf, nb, g))
        pl.when(sc[sel_b] == 1)(lambda: fill(bbuf, nb + 2, g))
        pl.when(sc[off] == 0)(lambda: product(g, 0))
        pl.when(sc[off] == 1)(lambda: product(g, 128))


def tri_in(sc, a_sets, b_sets, sel_a, off, sel_b):
    cb = 2
    ns = len(a_sets[0])

    def spec(arr, sel, want):
        shape = (cb,) + arr.shape[1:]
        if sel is None:
            return pl.BlockSpec(shape, lambda g, s: (g, 0, 0))
        return pl.BlockSpec(shape, lambda g, s: (jnp.where(s[sel] == want, g, 0), 0, 0))

    specs, args = [], []
    for k, group in enumerate(a_sets):
        specs += [spec(arr, sel_a, k // 2) for arr in group]
        args += list(group)
    for k, group in enumerate(b_sets):
        specs += [spec(arr, sel_b, k // 2) for arr in group]
        args += list(group)
    return pl.pallas_call(
        functools.partial(tri_in_kernel, ns, sel_a, off, sel_b),
        grid_spec=pltpu.PrefetchScalarGridSpec(
            num_scalar_prefetch=1, grid=(128 // cb,), in_specs=specs,
            out_specs=pl.BlockSpec((cb, 192, 384), lambda g, s: (g, 0, 0)),
            scratch_shapes=[pltpu.VMEM((768, 384), BF)] * 2),
        out_shape=jax.ShapeDtypeStruct((128, 192, 384), BF),
        compiler_params=params("arbitrary"), name="tri_in")(sc, *args)


def finish_kernel(sel, sc, t_ref, za_ref, zb_ref, n_ref, wg, wo, o_ref, st):
    stage_t(t_ref, st)
    half_a = sc[sel] == 0
    for i in range(0, IB, 2):
        zt = jnp.where(half_a, jnp.concatenate([za_ref[i], za_ref[i + 1]], axis=1),
                       jnp.concatenate([zb_ref[i], zb_ref[i + 1]], axis=1)).astype(F32)
        gate = dot(wg[...], norm_cols(zt, n_ref[4], n_ref[5]).astype(BF))
        upd = dot(wo[...], norm_cols(pair_t(st, i), n_ref[6], n_ref[7]).astype(BF))
        o = zt + (upd * jnp.tanh(gate) + upd)
        o_ref[i], o_ref[i + 1] = o[:, :128].T.astype(BF), o[:, 128:].T.astype(BF)


def finish(sc, row, sel, t, za, zb, norms, wg, wo):
    full = lambda a: pl.BlockSpec(a.shape, lambda i, j, s: (0,) * a.ndim)

    def zspec(want):
        def at(i, j, s):
            use = s[sel] == want
            return jnp.where(use, i, 0), 0, jnp.where(use, j, 0)
        return pl.BlockSpec((IB, 128, 128), at)

    return pl.pallas_call(
        functools.partial(finish_kernel, sel),
        grid_spec=pltpu.PrefetchScalarGridSpec(
            num_scalar_prefetch=1, grid=(96 // IB, 3),
            in_specs=[pl.BlockSpec((128, IB, 128), lambda i, j, s: (0, s[row] * (96 // IB) + i, j)),
                      zspec(0), zspec(1), full(norms), full(wg), full(wo)],
            out_specs=pl.BlockSpec((IB, 128, 128), lambda i, j, s: (i, j, 0)),
            scratch_shapes=[pltpu.VMEM((128 * ST, 128), F32)]),
        out_shape=jax.ShapeDtypeStruct((96, 384, 128), BF),
        compiler_params=params("arbitrary", "arbitrary"), name="finish")(sc, t, za, zb, norms, wg, wo)


def solution(mesh):
    row_spec = P(("data", "dap"), None, None)
    mask_spec = P(("data", "dap"), None)
    rep = P()

    chip_core = [(d // 2, d % 2) for d in range(8)]
    near = lambda chip, core: chip ^ (1 if core == 0 else 2)
    far = lambda chip, core: chip ^ (2 if core == 0 else 1)
    perm_x = [(near(p, c) * 2 + c, p * 2 + c) for p, c in chip_core]
    perm_w = [(far(p, c) * 2 + c, p * 2 + c) for p, c in chip_core]
    perm_d = [((p ^ 3) * 2 + c, p * 2 + c) for p, c in chip_core]
    perm_core = [(p * 2 + c, p * 2 + 1 - c) for p, c in chip_core]
    perm_a = [(p * 2 + 1 - p // 2, p * 2 + p // 2) for p in range(4)]
    perm_b = [(p * 2 + p // 2, p * 2 + 1 - p // 2) for p in range(4)]
    perm_cross = [(p * 2 + c, near(p, c) * 2 + 1 - c) for p, c in chip_core]
    perm_same = [(p * 2 + c, near(p, c) * 2 + c) for p, c in chip_core]
    send = lambda arr, perm: lax.ppermute(arr, "dap", perm)

    def per_device(z_one, mask_one, z_two, mask_two, norm_in, w_proj, w_gate, norm_mid, w_out):
        d = lax.axis_index("dap")
        core, chip = d % 2, d // 2
        x, y = chip % 2, chip // 2
        crop = (x + y) % 2
        i32 = lambda *v: jnp.stack([jnp.asarray(k, jnp.int32) for k in v])

        wide = lambda v, n: jnp.broadcast_to(v.astype(F32)[:, None], (128, n))
        norms = jnp.stack([wide(v, 256) for u in range(2) for v in
                           (norm_in[u, 0], norm_in[u, 1], norm_mid[u, 0], norm_mid[u, 1])])
        wp = [(w_proj[u].T * jnp.asarray(0.5, BF)) for u in range(2)]
        wg = [(w_gate[u].T * jnp.asarray(0.5, BF)) for u in range(2)]
        wo = [(w_out[u].T * jnp.asarray(0.5, BF)) for u in range(2)]

        first = crop == 0
        z_own, z_oth = jnp.where(first, z_one, z_two), jnp.where(first, z_two, z_one)
        m_own, m_oth = jnp.where(first, mask_one, mask_two), jnp.where(first, mask_two, mask_one)
        z_x, m_x = send(z_oth, perm_x), send(m_oth, perm_x)
        z_w, m_w = send(z_oth, perm_w), send(m_oth, perm_w)
        z_own_late, m_own_late, z_x, z_w = lax.optimization_barrier((z_own, m_own, z_x, z_w))
        z_d, m_d = send(z_own_late, perm_d), send(m_own_late, perm_d)

        pr = lambda z, m, total, off, prev=(): proj(z, m, norms[0], norms[1], wp[0], total, off, prev)
        a_o, b_o = pr(z_own, m_own, 96, 0)
        bo_o = send(b_o, perm_core)
        ab = pr(z_x, m_x, 192, 0)
        a_xw, b_xw = pr(z_w, m_w, 192, 96, ab)
        bo_xw = send(b_xw, perm_core)

        base = [x * 2 + core, x * 2 + 1 - core, (1 - x) * 2 + core, (1 - x) * 2 + 1 - core]
        sc_a = i32(*base, core, 1 - core)
        sc_b = i32(*base, 1 - core, core)
        t_a = tri_out(sc_a, [a_o, a_xw], [(b_o, None), (bo_o, None), (b_xw, 4), (bo_xw, 5)])

        sc_h = i32(y, 1 - y)
        md = lambda half, t, row, z, m: mid(sc_h, half, t, row, z, m, norms, wg[0], wo[0], wp[1])
        zs, am, bm = {}, {}, {}
        zs["oa"], am["oa"], bm["oa"] = md(0, t_a, 0, z_own, m_own)
        zs["xa"], am["xa"], bm["xa"] = md(0, t_a, 96, z_x, m_x)
        zs["wa"], am["wa"], bm["wa"] = md(0, t_a, 192, z_w, m_w)

        a_d, b_d = pr(z_d, m_d, 96, 0)
        bo_d = send(b_d, perm_core)
        t_b = tri_out(sc_b, [a_o, a_xw, a_d], [(b_xw, 4), (bo_xw, 5), (b_d, None), (bo_d, None)])
        t_da = tri_out(sc_a, [a_d], [(b_o, None), (bo_o, None), (b_xw, 4), (bo_xw, 5)])
        zs["ob"], am["ob"], bm["ob"] = md(1, t_b, 0, z_own, m_own)
        zs["xb"], am["xb"], bm["xb"] = md(1, t_b, 96, z_x, m_x)
        zs["wb"], am["wb"], bm["wb"] = md(1, t_b, 192, z_w, m_w)
        _, am["db"], bm["db"] = md(1, t_b, 288, z_d, m_d)
        _, am["da"], bm["da"] = md(0, t_da, 0, z_d, m_d)

        ao = {k: send(v, perm_core) for k, v in am.items()}
        bo = {k: send(v, perm_a if k[1] == "a" else perm_b) for k, v in bm.items()}
        zo = {k: send(zs[k], perm_a if k[1] == "a" else perm_b) for k in ("oa", "wa", "ob", "wb")}

        group = lambda arrs, h: [arrs[s + h] for s in "oxwd"]
        b_sets = [group(bm, "a"), group(bo, "a"), group(bm, "b"), group(bo, "b")]
        a_all = [group(am, "a"), group(ao, "a"), group(am, "b"), group(ao, "b")]
        keep_b = jnp.where(core == y, 0, 1)
        sc_i = i32(core, jnp.where(core == 0, 1 - x, x), x, keep_b, core, 1 - core)
        fin = lambda row, t, za, zb: finish(sc_i, row, 3, t, za, zb, norms, wg[1], wo[1])
        t_near = tri_in(sc_i, a_all, b_sets, 0, 1, 3)
        r_same = send(fin(4, t_near, zs["xa"], zs["xb"]), perm_same)
        r_cross = send(fin(5, t_near, zo["wa"], zo["wb"]), perm_cross)
        t_own = tri_in(sc_i, a_all[:2], b_sets, None, 2, 3)
        r_core = send(fin(5, t_own, zo["oa"], zo["ob"]), perm_core)
        r_keep = fin(4, t_own, zs["oa"], zs["ob"])

        lo_core = core == 0
        outs = []
        for own in (first, jnp.logical_not(first)):
            mine, yours = jnp.where(own, r_keep, r_same), jnp.where(own, r_core, r_cross)
            outs.append(jnp.concatenate([jnp.where(lo_core, mine, yours), jnp.where(lo_core, yours, mine)], axis=1))
        return tuple(outs)

    return jax.shard_map(per_device, mesh=mesh,
                         in_specs=(row_spec, mask_spec, row_spec, mask_spec, rep, rep, rep, rep, rep),
                         out_specs=(row_spec, row_spec), check_vma=False)
```

time: 3350 us -> 2120 us (0.63)
  Pallas kernels: 0 us -> 1070 us
  local copies, waits for them, and re-layouts: 961 us -> 7.42 us
  matrix products: 575 us -> 0 us
  waiting for transfers between devices: 1350 us -> 794 us
  other arithmetic: 391 us -> 71.6 us
  starting transfers between devices: 45.5 us -> 147 us
    all_to_all x8 -> x0, waiting for transfers between devices: 1350 us -> none  [the longest x4 845 us: tri_update(): sides_chan = lax.all_to_all(sides, 'dap', 1, 2, tiled=True)]
    pallas_call x0 -> x21, Pallas kernels: none -> 1070 us  [the longest x8 372 us: mid(): pl.pallas_call(mid_kernel, grid_spec=pltpu.PrefetchScalarGridSpec(num_sca...]
    ppermute x0 -> x32, waiting for transfers between devices: none -> 794 us  [solution(): send = lambda arr, perm: lax.ppermute(arr, 'dap', perm)]
    dot_general x16 -> x0, matrix products: 575 us -> none  [the longest x4 229 us: project_rows(): jnp.einsum('rnz,zsgc->sgcrn', x_norm, w_split, preferred_element_type=jnp...]
    convert_element_type x18 -> x0, local copies, waits for them, and re-layouts: 518 us -> none  [the longest x4 368 us: project_rows(): (keep_mask * jax.nn.sigmoid(projected[:, 1]) * projected[:, 0]).astype(jn...]
    convert_element_type x9 -> x2, other arithmetic: 290 us -> 0.01 us  [per_device(): wide = lambda v, n: jnp.broadcast_to(v.astype(F32)[:, None], (128, n))]
    slice x13 -> x3, local copies, waits for them, and re-layouts: 210 us -> 1.24 us  [the longest x1 0.61 us: per_device(): wg = [w_gate[u].T * jnp.asarray(0.5, BF) for u in range(2)]]
    ppermute x0 -> x32, starting transfers between devices: none -> 147 us  [solution(): send = lambda arr, perm: lax.ppermute(arr, 'dap', perm)]
  transfers between devices with their start and end apart: 8 -> 32, of which waited for: 8 -> 11; matrix products, arithmetic and copies ran while one was open for 33% -> 0% of each run, Pallas kernels for 0% -> 51%
where the time goes in v1:
time: 2120 us; the launch traced here: 2100 us
  Pallas kernels  1070 us (50%)
  waiting for transfers between devices  794 us (37%)
  starting transfers between devices  147 us (7%)
  other arithmetic  71.6 us (3%)
    ppermute x32, waiting for transfers between devices, solution(): send = lambda arr, perm: lax.ppermute(arr, 'dap', perm)  794 us
    pallas_call x8, Pallas kernels, mid(): pl.pallas_call(mid_kernel, grid_spec=pltpu.PrefetchScalarGridSpec(num_sca...  372 us
    pallas_call x3, Pallas kernels, tri_out(): pl.pallas_call(functools.partial(tri_out_kernel, len(lhs)), grid_spec=plt...  257 us
    pallas_call x2, Pallas kernels, tri_in(): pl.pallas_call(functools.partial(tri_in_kernel, ns, sel_a, off, sel_b), g...  193 us
    pallas_call x4, Pallas kernels, proj(): pl.pallas_call(proj_kernel, grid=(rows // IB, n // kb), in_specs=[pl.Bloc...  150 us
    ppermute x32, starting transfers between devices, solution(): send = lambda arr, perm: lax.ppermute(arr, 'dap', perm)  147 us
    pallas_call x4, Pallas kernels, finish(): pl.pallas_call(functools.partial(finish_kernel, sel), grid_spec=pltpu.Pre...  103 us
  transfers between devices with their start and end apart: 32, of which 11 were waited for; matrix products, arithmetic and copies ran while one was open for 0% of the time, Pallas kernels for 51%

profile of v1, /device:TPU:0, one launch (start us, length us, event | category | flops | bytes accessed | tf_op | source)
XLA Modules:
  0.0 2095.3 jit_solution(12098583378237627433)
XLA Ops:
  0.7 25.5 %broadcast_select_fusion = (bf16[96,768,128]{2,1,0:T(8,128)(2,1)}, bf16[96,768,128]{2,1,0:T(8,128)(2,1)}) fusion(bf16[96,768,128]{2,1,0:T(8,128)(2,1)} %param.11, bf16[96,768,128]{2,1,0:T(8,128)(2,1)} %param.9, pred[]{:T(512)S(6)} %eq.15), kind=kLoop, calls=%fused_computation.2 | loop fusion | flops 18874368 | bytes 75497472 | tf_op jit(solution)/shard_map/jit(_where)/select_n | solution.py:274
  32.6 402.5 %collective-permute-done.1.z_ref = bf16[96,768,128]{2,1,0:T(8,128)(2,1)} collective-permute-done((bf16[96,768,128]{2,1,0:T(8,128)(2,1)}, bf16[96,768,128]{2,1,0:T(8,128)(2,1)}, u32[]{:S(2)}, u32[]{:S(2)}) %collective-permute-start.1) | collective-permute-done | bytes 18874400 | tf_op jit(solution)/shard_map/ppermute | solution.py:257
  444.5 37.6 %proj.5 = (bf16[128,192,768]{2,1,0:T(8,128)(2,1)}, bf16[128,192,768]{2,1,0:T(8,128)(2,1)}) custom-call(bf16[96,768,128]{2,1,0:T(8,128)(2,1)} %collective-permute-done.z_ref, s32[96,768]{1,0:T(8,128)} %copy-done.4, f32[128,256]{1,0:T(8,128)} %squeeze.4.gain, f32[128,256]{1,0:T(8,128)} %squeeze.5.shift, bf16[512,128]{1,0:T(8,128)(2,1)} %multiply_bitcast_fusion.1.w_ref), custom_call_target="tpu_custom_call" | custom-call | tf_op jit(solution)/shard_map/proj/pallas_call | solution.py:61
  482.1 309.6 %collective-permute-done.2.m_ref = s32[96,768]{1,0:T(8,128)S(1)} collective-permute-done((s32[96,768]{1,0:T(8,128)S(1)}, s32[96,768]{1,0:T(8,128)S(1)}, u32[]{:S(2)}, u32[]{:S(2)}) %collective-permute-start.2) | collective-permute-done | bytes 294944 | tf_op jit(solution)/shard_map/ppermute | solution.py:257
  792.4 37.8 %proj.6 = (bf16[128,192,768]{2,1,0:T(8,128)(2,1)}, bf16[128,192,768]{2,1,0:T(8,128)(2,1)}) custom-call(bf16[96,768,128]{2,1,0:T(8,128)(2,1)} %collective-permute-done.1.z_ref, s32[96,768]{1,0:T(8,128)} %copy-done.3, f32[128,256]{1,0:T(8,128)} %squeeze.4.gain, f32[128,256]{1,0:T(8,128)} %squeeze.5.shift, ...), custom_call_target="tpu_custom_call", output_to_operand_aliasing={{0}: (5, {}), {1}: (6, {})} | custom-call | tf_op jit(solution)/shard_map/proj/pallas_call | solution.py:61
  830.2 78.3 %collective-permute-start.5 = (bf16[128,192,768]{2,1,0:T(8,128)(2,1)}, bf16[128,192,768]{2,1,0:T(8,128)(2,1)}, u32[]{:S(2)}, u32[]{:S(2)}) collective-permute-start(bf16[128,192,768]{2,1,0:T(8,128)(2,1)} %get-tuple-element.43), channel_id=1, source_target_pairs={{0,1},{1,0},{2,3},{3,2},{4,5},{5,4},{6,7},{7,6}} | collective-permute-start | bytes 113246216 | tf_op jit(solution)/shard_map/ppermute | solution.py:257
  908.5 10.1 collective-permute-done.7.m_ref
  919.4 37.5 %proj.7 = (bf16[128,96,768]{2,1,0:T(8,128)(2,1)}, bf16[128,96,768]{2,1,0:T(8,128)(2,1)}) custom-call(bf16[96,768,128]{2,1,0:T(8,128)(2,1)} %collective-permute-done.6.z_ref, s32[96,768]{1,0:T(8,128)} %copy-done.2, f32[128,256]{1,0:T(8,128)} %squeeze.4.gain, f32[128,256]{1,0:T(8,128)} %squeeze.5.shift, bf16[512,128]{1,0:T(8,128)(2,1)} %multiply_bitcast_fusion.1.w_ref), custom_call_target="tpu_custom_call" | custom-call | tf_op jit(solution)/shard_map/proj/pallas_call | solution.py:61
  956.9 37.5 %proj.4 = (bf16[128,96,768]{2,1,0:T(8,128)(2,1)}, bf16[128,96,768]{2,1,0:T(8,128)(2,1)}) custom-call(bf16[96,768,128]{2,1,0:T(8,128)(2,1)} %get-tuple-element.47.z_ref, s32[96,768]{1,0:T(8,128)} %copy-done.1, f32[128,256]{1,0:T(8,128)} %squeeze.4.gain, f32[128,256]{1,0:T(8,128)} %squeeze.5.shift, bf16[512,128]{1,0:T(8,128)(2,1)} %multiply_bitcast_fusion.1.w_ref), custom_call_target="tpu_custom_call" | custom-call | tf_op jit(solution)/shard_map/proj/pallas_call | solution.py:61
  1000.4 101.7 %tri_out.5.t_ref = bf16[128,384,384]{2,1,0:T(8,128)(2,1)} custom-call(s32[6]{0:T(128)} %stack.72.sc, bf16[128,96,768]{2,1,0:T(8,128)(2,1)} %get-tuple-element.36.refs_0_, bf16[128,192,768]{2,1,0:T(8,128)(2,1)} %get-tuple-element.41.refs_1_, bf16[128,96,768]{2,1,0:T(8,128)(2,1)} %get-tuple-element.49.refs_0_.refs_2_, bf16[128,2,96,768]{3,2,1,0:T(8,128)(2,1)} %bitcast.65, ...), custom_call_target="tpu_custom_call" | custom-call | tf_op jit(solution)/shard_map/tri_out/pallas_call | solution.py:95
  1102.1 46.5 %mid.15 = (bf16[96,128,384]{2,1,0:T(8,128)(2,1)}, bf16[128,96,384]{2,1,0:T(8,128)(2,1)}, bf16[128,96,384]{2,1,0:T(8,128)(2,1)}) custom-call(s32[2]{0:T(128)} %pad_add_fusion.sc, bf16[128,384,384]{2,1,0:T(8,128)(2,1)} %tri_out.5.t_ref, bf16[96,768,128]{2,1,0:T(8,128)(2,1)} %collective-permute-done.6.z_ref, s32[96,768]{1,0:T(8,128)} %copy-done.2, ...), custom_call_target="tpu_custom_call" | custom-call | tf_op jit(solution)/shard_map/mid/pallas_call | solution.py:139
  1154.5 66.1 %tri_out.4.t_ref = bf16[128,96,384]{2,1,0:T(8,128)(2,1)} custom-call(s32[6]{0:T(128)} %stack.70.sc, bf16[128,96,768]{2,1,0:T(8,128)(2,1)} %get-tuple-element.49.refs_0_.refs_2_, bf16[128,1,96,768]{3,2,1,0:T(8,128)(2,1)} %bitcast.68, bf16[128,1,96,768]{3,2,1,0:T(8,128)(2,1)} %bitcast.17.refs_3_.refs_2_, bf16[128,2,96,768]{3,2,1,0:T(8,128)(2,1)} %bitcast.66, ...), custom_call_target="tpu_custom_call" | custom-call | tf_op jit(solution)/shard_map/tri_out/pallas_call | solution.py:95
  1220.7 46.5 %mid.11 = (bf16[96,128,384]{2,1,0:T(8,128)(2,1)}, bf16[128,96,384]{2,1,0:T(8,128)(2,1)}, bf16[128,96,384]{2,1,0:T(8,128)(2,1)}) custom-call(s32[2]{0:T(128)} %pad_add_fusion.sc, bf16[128,96,384]{2,1,0:T(8,128)(2,1)} %tri_out.4.t_ref, bf16[96,768,128]{2,1,0:T(8,128)(2,1)} %collective-permute-done.6.z_ref, s32[96,768]{1,0:T(8,128)} %copy-done.2, ...), custom_call_target="tpu_custom_call" | custom-call | tf_op jit(solution)/shard_map/mid/pallas_call | solution.py:139
  1268.5 46.4 %mid.14 = (bf16[96,128,384]{2,1,0:T(8,128)(2,1)}, bf16[128,96,384]{2,1,0:T(8,128)(2,1)}, bf16[128,96,384]{2,1,0:T(8,128)(2,1)}) custom-call(s32[2]{0:T(128)} %pad_add_fusion.sc, bf16[128,384,384]{2,1,0:T(8,128)(2,1)} %tri_out.5.t_ref, bf16[96,768,128]{2,1,0:T(8,128)(2,1)} %collective-permute-done.1.z_ref, s32[96,768]{1,0:T(8,128)} %copy-done.3, ...), custom_call_target="tpu_custom_call" | custom-call | tf_op jit(solution)/shard_map/mid/pallas_call | solution.py:139
  1319.6 88.7 %tri_out.3.t_ref = bf16[128,288,384]{2,1,0:T(8,128)(2,1)} custom-call(s32[6]{0:T(128)} %stack.70.sc, bf16[128,96,768]{2,1,0:T(8,128)(2,1)} %get-tuple-element.36.refs_0_, bf16[128,192,768]{2,1,0:T(8,128)(2,1)} %get-tuple-element.41.refs_1_, bf16[128,1,96,768]{3,2,1,0:T(8,128)(2,1)} %bitcast.69, bf16[128,1,96,768]{3,2,1,0:T(8,128)(2,1)} %bitcast.17.refs_3_.refs_2_, ...), custom_call_target="tpu_custom_call" | custom-call | tf_op jit(solution)/shard_map/tri_out/pallas_call | solution.py:95
  1408.3 46.4 %mid.12 = (bf16[96,128,384]{2,1,0:T(8,128)(2,1)}, bf16[128,96,384]{2,1,0:T(8,128)(2,1)}, bf16[128,96,384]{2,1,0:T(8,128)(2,1)}) custom-call(s32[2]{0:T(128)} %pad_add_fusion.sc, bf16[128,384,384]{2,1,0:T(8,128)(2,1)} %tri_out.5.t_ref, bf16[96,768,128]{2,1,0:T(8,128)(2,1)} %get-tuple-element.47.z_ref, s32[96,768]{1,0:T(8,128)} %copy-done.1, ...), custom_call_target="tpu_custom_call" | custom-call | tf_op jit(solution)/shard_map/mid/pallas_call | solution.py:139
  1460.4 46.7 %mid.13 = (bf16[96,128,384]{2,1,0:T(8,128)(2,1)}, bf16[128,96,384]{2,1,0:T(8,128)(2,1)}, bf16[128,96,384]{2,1,0:T(8,128)(2,1)}) custom-call(s32[2]{0:T(128)} %pad_add_fusion.sc, bf16[128,384,384]{2,1,0:T(8,128)(2,1)} %tri_out.5.t_ref, bf16[96,768,128]{2,1,0:T(8,128)(2,1)} %collective-permute-done.z_ref, s32[96,768]{1,0:T(8,128)} %copy-done.4, ...), custom_call_target="tpu_custom_call" | custom-call | tf_op jit(solution)/shard_map/mid/pallas_call | solution.py:139
  1507.0 46.4 %mid.10 = (bf16[96,128,384]{2,1,0:T(8,128)(2,1)}, bf16[128,96,384]{2,1,0:T(8,128)(2,1)}, bf16[128,96,384]{2,1,0:T(8,128)(2,1)}) custom-call(s32[2]{0:T(128)} %pad_add_fusion.sc, bf16[128,288,384]{2,1,0:T(8,128)(2,1)} %tri_out.3.t_ref, bf16[96,768,128]{2,1,0:T(8,128)(2,1)} %collective-permute-done.1.z_ref, s32[96,768]{1,0:T(8,128)} %copy-done.3, ...), custom_call_target="tpu_custom_call" | custom-call | tf_op jit(solution)/shard_map/mid/pallas_call | solution.py:139
  1565.5 46.3 %mid.8 = (bf16[96,128,384]{2,1,0:T(8,128)(2,1)}, bf16[128,96,384]{2,1,0:T(8,128)(2,1)}, bf16[128,96,384]{2,1,0:T(8,128)(2,1)}) custom-call(s32[2]{0:T(128)} %pad_add_fusion.sc, bf16[128,288,384]{2,1,0:T(8,128)(2,1)} %tri_out.3.t_ref, bf16[96,768,128]{2,1,0:T(8,128)(2,1)} %get-tuple-element.47.z_ref, s32[96,768]{1,0:T(8,128)} %copy-done.1, ...), custom_call_target="tpu_custom_call" | custom-call | tf_op jit(solution)/shard_map/mid/pallas_call | solution.py:139
  1611.9 46.5 %mid.9 = (bf16[96,128,384]{2,1,0:T(8,128)(2,1)}, bf16[128,96,384]{2,1,0:T(8,128)(2,1)}, bf16[128,96,384]{2,1,0:T(8,128)(2,1)}) custom-call(s32[2]{0:T(128)} %pad_add_fusion.sc, bf16[128,288,384]{2,1,0:T(8,128)(2,1)} %tri_out.3.t_ref, bf16[96,768,128]{2,1,0:T(8,128)(2,1)} %collective-permute-done.z_ref, s32[96,768]{1,0:T(8,128)} %copy-done.4, ...), custom_call_target="tpu_custom_call" | custom-call | tf_op jit(solution)/shard_map/mid/pallas_call | solution.py:139
  1691.3 7.6 collective-permute-start.27
  1707.7 10.6 collective-permute-done.13.refs_13_.refs_21_
  1718.3 102.8 %tri_in.3.t_ref = bf16[128,192,384]{2,1,0:T(8,128)(2,1)} custom-call(s32[6]{0:T(128)} %stack.62.sc, bf16[128,96,384]{2,1,0:T(8,128)(2,1)} %get-tuple-element.44.refs_0_, bf16[128,96,384]{2,1,0:T(8,128)(2,1)} %get-tuple-element.45.refs_1_, bf16[128,96,384]{2,1,0:T(8,128)(2,1)} %get-tuple-element.46.refs_2_, bf16[128,96,384]{2,1,0:T(8,128)(2,1)} %get-tuple-element.50.refs_3_, ...), custom_call_target="tpu_custom_call" | custom-call | tf_op jit(solution)/shard_map/tri_in/pallas_call | solution.py:198
  1821.2 25.7 %finish.5 = bf16[96,384,128]{2,1,0:T(8,128)(2,1)} custom-call(s32[6]{0:T(128)} %stack.62.sc, bf16[128,192,384]{2,1,0:T(8,128)(2,1)} %tri_in.3.t_ref, bf16[96,128,384]{2,1,0:T(8,128)(2,1)} %get-tuple-element.66.za_ref, bf16[96,128,384]{2,1,0:T(8,128)(2,1)} %get-tuple-element.67.zb_ref, f32[8,128,256]{2,1,0:T(8,128)} %copy-done, ...), custom_call_target="tpu_custom_call" | custom-call | tf_op jit(solution)/shard_map/finish/pallas_call | solution.py:229
  1847.1 25.7 %finish.7 = bf16[96,384,128]{2,1,0:T(8,128)(2,1)} custom-call(s32[6]{0:T(128)} %stack.62.sc, bf16[128,192,384]{2,1,0:T(8,128)(2,1)} %tri_in.3.t_ref, bf16[96,128,384]{2,1,0:T(8,128)(2,1)} %collective-permute-done.29.za_ref, bf16[96,128,384]{2,1,0:T(8,128)(2,1)} %collective-permute-done.30.zb_ref, f32[8,128,256]{2,1,0:T(8,128)} %copy-done, ...), custom_call_target="tpu_custom_call" | custom-call | tf_op jit(solution)/shard_map/finish/pallas_call | solution.py:229
  1873.2 89.9 %tri_in.2.t_ref = bf16[128,192,384]{2,1,0:T(8,128)(2,1)} custom-call(s32[6]{0:T(128)} %stack.62.sc, bf16[128,96,384]{2,1,0:T(8,128)(2,1)} %get-tuple-element.44.refs_0_, bf16[128,96,384]{2,1,0:T(8,128)(2,1)} %get-tuple-element.45.refs_1_, bf16[128,96,384]{2,1,0:T(8,128)(2,1)} %get-tuple-element.46.refs_2_, bf16[128,96,384]{2,1,0:T(8,128)(2,1)} %get-tuple-element.50.refs_3_, ...), custom_call_target="tpu_custom_call" | custom-call | tf_op jit(solution)/shard_map/tri_in/pallas_call | solution.py:198
  1963.1 25.7 %finish.6 = bf16[96,384,128]{2,1,0:T(8,128)(2,1)} custom-call(s32[6]{0:T(128)} %stack.62.sc, bf16[128,192,384]{2,1,0:T(8,128)(2,1)} %tri_in.2.t_ref, bf16[96,128,384]{2,1,0:T(8,128)(2,1)} %collective-permute-done.26.za_ref, bf16[96,128,384]{2,1,0:T(8,128)(2,1)} %collective-permute-done.27.zb_ref, f32[8,128,256]{2,1,0:T(8,128)} %copy-done, ...), custom_call_target="tpu_custom_call" | custom-call | tf_op jit(solution)/shard_map/finish/pallas_call | solution.py:229
  1990.8 25.7 %finish.4 = bf16[96,384,128]{2,1,0:T(8,128)(2,1)} custom-call(s32[6]{0:T(128)} %stack.62.sc, bf16[128,192,384]{2,1,0:T(8,128)(2,1)} %tri_in.2.t_ref, bf16[96,128,384]{2,1,0:T(8,128)(2,1)} %get-tuple-element.60.za_ref, bf16[96,128,384]{2,1,0:T(8,128)(2,1)} %get-tuple-element.61.zb_ref, f32[8,128,256]{2,1,0:T(8,128)} %copy-done, ...), custom_call_target="tpu_custom_call" | custom-call | tf_op jit(solution)/shard_map/finish/pallas_call | solution.py:229
  2016.5 35.6 %collective-permute-done.31 = bf16[96,384,128]{2,1,0:T(8,128)(2,1)} collective-permute-done((bf16[96,384,128]{2,1,0:T(8,128)(2,1)}, bf16[96,384,128]{2,1,0:T(8,128)(2,1)}, u32[]{:S(2)}, u32[]{:S(2)}) %collective-permute-start.31) | collective-permute-done | bytes 9437216 | tf_op jit(solution)/shard_map/ppermute | solution.py:257
  2052.1 16.2 broadcast_select_fusion.7
  2068.3 14.5 pad_maximum_fusion.1
  2082.9 12.0 pad_maximum_fusion
  (115 shorter events, 96.8 us)
Async XLA Ops:
  26.3 408.8 %collective-permute-start.1 = (bf16[96,768,128]{2,1,0:T(8,128)(2,1)}, bf16[96,768,128]{2,1,0:T(8,128)(2,1)}, u32[]{:S(2)}, u32[]{:S(2)}) collective-permute-start(bf16[96,768,128]{2,1,0:T(8,128)(2,1)} %get-tuple-element.74), channel_id=1, source_target_pairs={{4,0},{3,1},{6,2},{1,3},{0,4},{7,5},{2,6},{5,7}} | collective-permute-start | bytes 56623112 | tf_op jit(solution)/shard_map/ppermute | solution.py:257
  29.6 408.0 %collective-permute-start = (bf16[96,768,128]{2,1,0:T(8,128)(2,1)}, bf16[96,768,128]{2,1,0:T(8,128)(2,1)}, u32[]{:S(2)}, u32[]{:S(2)}) collective-permute-start(bf16[96,768,128]{2,1,0:T(8,128)(2,1)} %get-tuple-element.74), channel_id=1, source_target_pairs={{2,0},{5,1},{0,2},{7,3},{6,4},{1,5},{4,6},{3,7}} | collective-permute-start | bytes 56623112 | tf_op jit(solution)/shard_map/ppermute | solution.py:257
  31.2 411.8 %collective-permute-start.3 = (s32[96,768]{1,0:T(8,128)S(1)}, s32[96,768]{1,0:T(8,128)S(1)}, u32[]{:S(2)}, u32[]{:S(2)}) collective-permute-start(s32[96,768]{1,0:T(8,128)S(1)} %get-tuple-element.76), channel_id=1, source_target_pairs={{2,0},{5,1},{0,2},{7,3},{6,4},{1,5},{4,6},{3,7}} | collective-permute-start | bytes 884744 | tf_op jit(solution)/shard_map/ppermute | solution.py:257
  31.7 760.0 %collective-permute-start.2 = (s32[96,768]{1,0:T(8,128)S(1)}, s32[96,768]{1,0:T(8,128)S(1)}, u32[]{:S(2)}, u32[]{:S(2)}) collective-permute-start(s32[96,768]{1,0:T(8,128)S(1)} %get-tuple-element.76), channel_id=1, source_target_pairs={{4,0},{3,1},{6,2},{1,3},{0,4},{7,5},{2,6},{5,7}} | collective-permute-start | bytes 884744 | tf_op jit(solution)/shard_map/ppermute | solution.py:257
  437.7 481.0 %collective-permute-start.6 = (bf16[96,768,128]{2,1,0:T(8,128)(2,1)}, bf16[96,768,128]{2,1,0:T(8,128)(2,1)}, u32[]{:S(2)}, u32[]{:S(2)}) collective-permute-start(bf16[96,768,128]{2,1,0:T(8,128)(2,1)} %get-tuple-element.47.z_ref), channel_id=1, source_target_pairs={{6,0},{7,1},{4,2},{5,3},{2,4},{3,5},{0,6},{1,7}} | collective-permute-start | bytes 56623112 | tf_op jit(solution)/shard_map/ppermute | solution.py:257
  830.2 170.1 %collective-permute-start.5 = (bf16[128,192,768]{2,1,0:T(8,128)(2,1)}, bf16[128,192,768]{2,1,0:T(8,128)(2,1)}, u32[]{:S(2)}, u32[]{:S(2)}) collective-permute-start(bf16[128,192,768]{2,1,0:T(8,128)(2,1)} %get-tuple-element.43), channel_id=1, source_target_pairs={{0,1},{1,0},{2,3},{3,2},{4,5},{5,4},{6,7},{7,6}} | collective-permute-start | bytes 113246216 | tf_op jit(solution)/shard_map/ppermute | solution.py:257
  908.5 10.1 collective-permute-start.7
  956.9 43.5 %collective-permute-start.16 = (bf16[128,96,768]{2,1,0:T(8,128)(2,1)}, bf16[128,96,768]{2,1,0:T(8,128)(2,1)}, u32[]{:S(2)}, u32[]{:S(2)}) collective-permute-start(bf16[128,96,768]{2,1,0:T(8,128)(2,1)} %get-tuple-element.55), channel_id=1, source_target_pairs={{0,1},{1,0},{2,3},{3,2},{4,5},{5,4},{6,7},{7,6}} | collective-permute-start | bytes 56623112 | tf_op jit(solution)/shard_map/ppermute | solution.py:257
  994.4 160.1 %collective-permute-start.4 = (bf16[128,96,768]{2,1,0:T(8,128)(2,1)}, bf16[128,96,768]{2,1,0:T(8,128)(2,1)}, u32[]{:S(2)}, u32[]{:S(2)}) collective-permute-start(bf16[128,96,768]{2,1,0:T(8,128)(2,1)} %get-tuple-element.42), channel_id=1, source_target_pairs={{0,1},{1,0},{2,3},{3,2},{4,5},{5,4},{6,7},{7,6}} | collective-permute-start | bytes 56623112 | tf_op jit(solution)/shard_map/ppermute | solution.py:257
  1148.6 306.1 %collective-permute-start.24 = (bf16[128,96,384]{2,1,0:T(8,128)(2,1)}, bf16[128,96,384]{2,1,0:T(8,128)(2,1)}, u32[]{:S(2)}, u32[]{:S(2)}) collective-permute-start(bf16[128,96,384]{2,1,0:T(8,128)(2,1)} %get-tuple-element.65.refs_11_), channel_id=1, source_target_pairs={{0,1},{1,0},{2,3},{3,2},{4,5},{5,4},{6,7},{7,6}} | collective-permute-start | bytes 28311560 | tf_op jit(solution)/shard_map/ppermute | solution.py:257
  1148.8 404.7 %collective-permute-start.20 = (bf16[128,96,384]{2,1,0:T(8,128)(2,1)}, bf16[128,96,384]{2,1,0:T(8,128)(2,1)}, u32[]{:S(2)}, u32[]{:S(2)}) collective-permute-start(bf16[128,96,384]{2,1,0:T(8,128)(2,1)} %get-tuple-element.59.refs_19_.refs_27_), channel_id=1, source_target_pairs={{0,1},{2,3},{5,4},{7,6}} | collective-permute-start | bytes 28311560 | tf_op jit(solution)/shard_map/ppermute | solution.py:257
  1267.2 286.3 %collective-permute-start.11 = (bf16[128,96,384]{2,1,0:T(8,128)(2,1)}, bf16[128,96,384]{2,1,0:T(8,128)(2,1)}, u32[]{:S(2)}, u32[]{:S(2)}) collective-permute-start(bf16[128,96,384]{2,1,0:T(8,128)(2,1)} %get-tuple-element.50.refs_3_), channel_id=1, source_target_pairs={{0,1},{1,0},{2,3},{3,2},{4,5},{5,4},{6,7},{7,6}} | collective-permute-start | bytes 28311560 | tf_op jit(solution)/shard_map/ppermute | solution.py:257
  1267.2 287.6 %collective-permute-start.15 = (bf16[128,96,384]{2,1,0:T(8,128)(2,1)}, bf16[128,96,384]{2,1,0:T(8,128)(2,1)}, u32[]{:S(2)}, u32[]{:S(2)}) collective-permute-start(bf16[128,96,384]{2,1,0:T(8,128)(2,1)} %get-tuple-element.54.refs_11_.refs_19_), channel_id=1, source_target_pairs={{1,0},{3,2},{4,5},{6,7}} | collective-permute-start | bytes 28311560 | tf_op jit(solution)/shard_map/ppermute | solution.py:257
  1314.8 244.7 %collective-permute-start.23 = (bf16[128,96,384]{2,1,0:T(8,128)(2,1)}, bf16[128,96,384]{2,1,0:T(8,128)(2,1)}, u32[]{:S(2)}, u32[]{:S(2)}) collective-permute-start(bf16[128,96,384]{2,1,0:T(8,128)(2,1)} %get-tuple-element.64.refs_10_), channel_id=1, source_target_pairs={{0,1},{1,0},{2,3},{3,2},{4,5},{5,4},{6,7},{7,6}} | collective-permute-start | bytes 28311560 | tf_op jit(solution)/shard_map/ppermute | solution.py:257
  1454.7 104.9 %collective-permute-start.19 = (bf16[128,96,384]{2,1,0:T(8,128)(2,1)}, bf16[128,96,384]{2,1,0:T(8,128)(2,1)}, u32[]{:S(2)}, u32[]{:S(2)}) collective-permute-start(bf16[128,96,384]{2,1,0:T(8,128)(2,1)} %get-tuple-element.58.refs_18_.refs_26_), channel_id=1, source_target_pairs={{0,1},{2,3},{5,4},{7,6}} | collective-permute-start | bytes 28311560 | tf_op jit(solution)/shard_map/ppermute | solution.py:257
  1553.4 105.0 %collective-permute-start.10 = (bf16[128,96,384]{2,1,0:T(8,128)(2,1)}, bf16[128,96,384]{2,1,0:T(8,128)(2,1)}, u32[]{:S(2)}, u32[]{:S(2)}) collective-permute-start(bf16[128,96,384]{2,1,0:T(8,128)(2,1)} %get-tuple-element.46.refs_2_), channel_id=1, source_target_pairs={{0,1},{1,0},{2,3},{3,2},{4,5},{5,4},{6,7},{7,6}} | collective-permute-start | bytes 28311560 | tf_op jit(solution)/shard_map/ppermute | solution.py:257
  1553.5 109.7 %collective-permute-start.14 = (bf16[128,96,384]{2,1,0:T(8,128)(2,1)}, bf16[128,96,384]{2,1,0:T(8,128)(2,1)}, u32[]{:S(2)}, u32[]{:S(2)}) collective-permute-start(bf16[128,96,384]{2,1,0:T(8,128)(2,1)} %get-tuple-element.53.refs_10_.refs_18_), channel_id=1, source_target_pairs={{1,0},{3,2},{4,5},{6,7}} | collective-permute-start | bytes 28311560 | tf_op jit(solution)/shard_map/ppermute | solution.py:257
  1554.8 108.4 %collective-permute-start.21 = (bf16[128,96,384]{2,1,0:T(8,128)(2,1)}, bf16[128,96,384]{2,1,0:T(8,128)(2,1)}, u32[]{:S(2)}, u32[]{:S(2)}) collective-permute-start(bf16[128,96,384]{2,1,0:T(8,128)(2,1)} %get-tuple-element.62.refs_8_), channel_id=1, source_target_pairs={{0,1},{1,0},{2,3},{3,2},{4,5},{5,4},{6,7},{7,6}} | collective-permute-start | bytes 28311560 | tf_op jit(solution)/shard_map/ppermute | solution.py:257
  1559.5 105.0 %collective-permute-start.22 = (bf16[128,96,384]{2,1,0:T(8,128)(2,1)}, bf16[128,96,384]{2,1,0:T(8,128)(2,1)}, u32[]{:S(2)}, u32[]{:S(2)}) collective-permute-start(bf16[128,96,384]{2,1,0:T(8,128)(2,1)} %get-tuple-element.63.refs_9_), channel_id=1, source_target_pairs={{0,1},{1,0},{2,3},{3,2},{4,5},{5,4},{6,7},{7,6}} | collective-permute-start | bytes 28311560 | tf_op jit(solution)/shard_map/ppermute | solution.py:257
  1559.6 109.6 %collective-permute-start.17 = (bf16[128,96,384]{2,1,0:T(8,128)(2,1)}, bf16[128,96,384]{2,1,0:T(8,128)(2,1)}, u32[]{:S(2)}, u32[]{:S(2)}) collective-permute-start(bf16[128,96,384]{2,1,0:T(8,128)(2,1)} %get-tuple-element.56.refs_16_.refs_24_), channel_id=1, source_target_pairs={{0,1},{2,3},{5,4},{7,6}} | collective-permute-start | bytes 28311560 | tf_op jit(solution)/shard_map/ppermute | solution.py:257
  1658.4 15.6 collective-permute-start.18
  1663.2 24.3 %collective-permute-start.8 = (bf16[128,96,384]{2,1,0:T(8,128)(2,1)}, bf16[128,96,384]{2,1,0:T(8,128)(2,1)}, u32[]{:S(2)}, u32[]{:S(2)}) collective-permute-start(bf16[128,96,384]{2,1,0:T(8,128)(2,1)} %get-tuple-element.44.refs_0_), channel_id=1, source_target_pairs={{0,1},{1,0},{2,3},{3,2},{4,5},{5,4},{6,7},{7,6}} | collective-permute-start | bytes 28311560 | tf_op jit(solution)/shard_map/ppermute | solution.py:257
  1663.2 28.1 %collective-permute-start.12 = (bf16[128,96,384]{2,1,0:T(8,128)(2,1)}, bf16[128,96,384]{2,1,0:T(8,128)(2,1)}, u32[]{:S(2)}, u32[]{:S(2)}) collective-permute-start(bf16[128,96,384]{2,1,0:T(8,128)(2,1)} %get-tuple-element.51.refs_8_.refs_16_), channel_id=1, source_target_pairs={{1,0},{3,2},{4,5},{6,7}} | collective-permute-start | bytes 28311560 | tf_op jit(solution)/shard_map/ppermute | solution.py:257
  1664.5 40.3 %collective-permute-start.9 = (bf16[128,96,384]{2,1,0:T(8,128)(2,1)}, bf16[128,96,384]{2,1,0:T(8,128)(2,1)}, u32[]{:S(2)}, u32[]{:S(2)}) collective-permute-start(bf16[128,96,384]{2,1,0:T(8,128)(2,1)} %get-tuple-element.45.refs_1_), channel_id=1, source_target_pairs={{0,1},{1,0},{2,3},{3,2},{4,5},{5,4},{6,7},{7,6}} | collective-permute-start | bytes 28311560 | tf_op jit(solution)/shard_map/ppermute | solution.py:257
  1669.2 49.1 %collective-permute-start.13 = (bf16[128,96,384]{2,1,0:T(8,128)(2,1)}, bf16[128,96,384]{2,1,0:T(8,128)(2,1)}, u32[]{:S(2)}, u32[]{:S(2)}) collective-permute-start(bf16[128,96,384]{2,1,0:T(8,128)(2,1)} %get-tuple-element.52.refs_9_.refs_17_), channel_id=1, source_target_pairs={{1,0},{3,2},{4,5},{6,7}} | collective-permute-start | bytes 28311560 | tf_op jit(solution)/shard_map/ppermute | solution.py:257
  1674.0 173.1 %collective-permute-start.30 = (bf16[96,128,384]{2,1,0:T(8,128)(2,1)}, bf16[96,128,384]{2,1,0:T(8,128)(2,1)}, u32[]{:S(2)}, u32[]{:S(2)}) collective-permute-start(bf16[96,128,384]{2,1,0:T(8,128)(2,1)} %get-tuple-element.69), channel_id=1, source_target_pairs={{0,1},{2,3},{5,4},{7,6}} | collective-permute-start | bytes 28311560 | tf_op jit(solution)/shard_map/ppermute | solution.py:257
  1687.5 159.6 %collective-permute-start.29 = (bf16[96,128,384]{2,1,0:T(8,128)(2,1)}, bf16[96,128,384]{2,1,0:T(8,128)(2,1)}, u32[]{:S(2)}, u32[]{:S(2)}) collective-permute-start(bf16[96,128,384]{2,1,0:T(8,128)(2,1)} %get-tuple-element.68), channel_id=1, source_target_pairs={{1,0},{3,2},{4,5},{6,7}} | collective-permute-start | bytes 28311560 | tf_op jit(solution)/shard_map/ppermute | solution.py:257
  1691.3 271.8 %collective-permute-start.27 = (bf16[96,128,384]{2,1,0:T(8,128)(2,1)}, bf16[96,128,384]{2,1,0:T(8,128)(2,1)}, u32[]{:S(2)}, u32[]{:S(2)}) collective-permute-start(bf16[96,128,384]{2,1,0:T(8,128)(2,1)} %get-tuple-element.61.zb_ref), channel_id=1, source_target_pairs={{0,1},{2,3},{5,4},{7,6}} | collective-permute-start | bytes 28311560 | tf_op jit(solution)/shard_map/ppermute | solution.py:257
  1704.8 258.3 %collective-permute-start.26 = (bf16[96,128,384]{2,1,0:T(8,128)(2,1)}, bf16[96,128,384]{2,1,0:T(8,128)(2,1)}, u32[]{:S(2)}, u32[]{:S(2)}) collective-permute-start(bf16[96,128,384]{2,1,0:T(8,128)(2,1)} %get-tuple-element.60.za_ref), channel_id=1, source_target_pairs={{1,0},{3,2},{4,5},{6,7}} | collective-permute-start | bytes 28311560 | tf_op jit(solution)/shard_map/ppermute | solution.py:257
  1846.9 169.6 %collective-permute-start.25 = (bf16[96,384,128]{2,1,0:T(8,128)(2,1)}, bf16[96,384,128]{2,1,0:T(8,128)(2,1)}, u32[]{:S(2)}, u32[]{:S(2)}) collective-permute-start(bf16[96,384,128]{2,1,0:T(8,128)(2,1)} %finish.5), channel_id=1, source_target_pairs={{0,2},{1,5},{2,0},{3,7},{4,6},{5,1},{6,4},{7,3}} | collective-permute-start | bytes 28311560 | tf_op jit(solution)/shard_map/ppermute | solution.py:257
  1872.8 179.3 %collective-permute-start.31 = (bf16[96,384,128]{2,1,0:T(8,128)(2,1)}, bf16[96,384,128]{2,1,0:T(8,128)(2,1)}, u32[]{:S(2)}, u32[]{:S(2)}) collective-permute-start(bf16[96,384,128]{2,1,0:T(8,128)(2,1)} %finish.7), channel_id=1, source_target_pairs={{0,3},{1,4},{2,1},{3,6},{4,7},{5,0},{6,5},{7,2}} | collective-permute-start | bytes 28311560 | tf_op jit(solution)/shard_map/ppermute | solution.py:257
  1988.9 63.3 %collective-permute-start.28 = (bf16[96,384,128]{2,1,0:T(8,128)(2,1)}, bf16[96,384,128]{2,1,0:T(8,128)(2,1)}, u32[]{:S(2)}, u32[]{:S(2)}) collective-permute-start(bf16[96,384,128]{2,1,0:T(8,128)(2,1)} %finish.6), channel_id=1, source_target_pairs={{0,1},{1,0},{2,3},{3,2},{4,5},{5,4},{6,7},{7,6}} | collective-permute-start | bytes 28311560 | tf_op jit(solution)/shard_map/ppermute | solution.py:257
  (14 other events, 1415.2 us)
